TPU v7x, 32 devices: a whole 2x2x4 slice. The times are simulated.
32 devices in a mesh: row: 4 (over y, core), col: 8 (over z, x).
Axes of the slice: x: 2, y: 2, z: 4, core: 2. Of those that a mesh axis runs over, the one named last changes fastest.
Arguments:
- adjacency: int32 [8192, 8192], P('row', 'col'), may hold values from 0 to 1, as said below
Outputs:
- closure: bfloat16 [8192, 8192], P('row', 'col')
Inputs may be any that keep to these rules, and one draw needn't show every extreme that they name: `adjacency`: every entry is 0 or 1; there is no bound on the number of ones in a row, a column or a block, and their share differs widely between rows and between columns.
All inputs are finite; a program needn't handle non-finite values.
Results may differ from a plain program's by a relative error of at most 0.001.
Values may be sent and summed in bfloat16 or wider, within the bound.
A program may use at most 192 MiB of HBM per device.

v0:
```python
import functools

import jax
import jax.numpy as jnp
from jax import lax
from jax.experimental import pallas as pl
from jax.experimental.pallas import tpu as pltpu
from jax.sharding import PartitionSpec as P

PANEL = 512
PANELS = 4

CHUNK = 32
RIGHT = 64
GROUP = 256
TAIL = 128
TILE = 512
PER_STEP = 1
MESH = pl.DeviceIdType.MESH


def lag_of(row):
    return 1 + (5 * row) // 2


def kernel(n_rows, n_cols, window, adj_hbm, out, adj, left, right, partial,
           adj_sem, z_send, b_send, z_recv, x_send, x_recv, r_send, r_recv):
    block_rows, block_cols = adj.shape
    holders = left.shape[0]
    stages = n_cols // holders
    n_chunks = block_rows // CHUNK
    n_adj = block_rows // RIGHT
    n_right = window // RIGHT
    n_groups = block_rows // GROUP
    n_tiles = block_cols // TILE
    units = n_groups * n_tiles
    per_group = GROUP // CHUNK

    r = lax.axis_index("row")
    c = lax.axis_index("col")
    hi = c // holders
    lo = lax.rem(c, holders)
    lag = lag_of(r)

    relay = lax.rem(hi, 2) == 0
    feeds_next = relay & (hi < stages - 1)
    feeds_back = relay & (hi > 0)
    next_col = c + holders * (1 + (hi + 2 < stages).astype(jnp.int32))
    back_col = c - holders

    def adj_copy(i):
        rows = pl.ds(pl.multiple_of(i * RIGHT, RIGHT), RIGHT)
        return pltpu.make_async_copy(adj_hbm.at[rows], adj.at[rows], adj_sem.at[i])

    def chunk(j):
        return pl.ds(pl.multiple_of(j * CHUNK, CHUNK), CHUNK)

    def z_copy(j):
        part = left.at[lo, chunk(j)]
        return pltpu.make_async_remote_copy(
            src_ref=part, dst_ref=part, send_sem=z_send, recv_sem=z_recv.at[j],
            device_id={"col": next_col}, device_id_type=MESH)

    def z_back(j):
        part = left.at[lo, chunk(j)]
        return pltpu.make_async_remote_copy(
            src_ref=part, dst_ref=part, send_sem=b_send, recv_sem=z_recv.at[j],
            device_id={"col": back_col}, device_id_type=MESH)

    def x_copy(d, j):
        part = left.at[lo, chunk(j)]
        peer = hi * holders + lax.rem(lo + d, holders)
        return pltpu.make_async_remote_copy(
            src_ref=part, dst_ref=part, send_sem=x_send.at[d - 1], recv_sem=x_recv.at[d - 1, j],
            device_id={"col": peer}, device_id_type=MESH)

    def x_arrival(d, j):
        part = left.at[lax.rem(lo + holders - d, holders), chunk(j)]
        peer = hi * holders + lax.rem(lo + holders - d, holders)
        return pltpu.make_async_remote_copy(
            src_ref=part, dst_ref=part, send_sem=x_send.at[d - 1], recv_sem=x_recv.at[d - 1, j],
            device_id={"col": peer}, device_id_type=MESH)

    def r_rows(i):
        return pl.ds(pl.multiple_of(i * RIGHT, RIGHT), RIGHT)

    def r_copy(i):
        part = right.at[r_rows(i)]
        return pltpu.make_async_remote_copy(
            src_ref=part, dst_ref=part, send_sem=r_send, recv_sem=r_recv.at[i],
            device_id={"row": r + 1}, device_id_type=MESH)

    adj_copy(0).start()

    barrier = pltpu.get_barrier_semaphore()

    def greet(where):
        pl.semaphore_signal(barrier, inc=1, device_id=where, device_id_type=MESH)

    @pl.when(feeds_back)
    def _():
        greet({"col": c - 2 * holders})
        greet({"col": back_col})

    @pl.when(feeds_next)
    def _():
        greet({"col": next_col})

    @pl.when(~relay & (hi < stages - 1))
    def _():
        greet({"col": c + holders})

    @pl.when(~relay & (hi == stages - 1))
    def _():
        greet({"col": c - holders})

    for d in range(1, holders):
        greet({"col": hi * holders + lax.rem(lo + d, holders)})

    @pl.when(r > 0)
    def _():
        greet({"row": r - 1})

    @pl.when(r < n_rows - 1)
    def _():
        greet({"row": r + 1})

    def convert_left(j):
        left[lo, chunk(j), :] = adj[chunk(j), :].astype(jnp.bfloat16)

    def convert_right(i):
        right[r_rows(i), :] = adj[r_rows(i), :].astype(jnp.bfloat16)

    ahead = RIGHT // CHUNK
    adj_copy(0).wait()

    @pl.loop(1, n_adj)
    def _(i):
        adj_copy(i).start()

    @pl.when(hi == 0)
    def _():
        for k in range(ahead):
            convert_left(k)

    @pl.when(r == 0)
    def _():
        convert_right(0)

    known = (2 * feeds_back.astype(jnp.int32) + feeds_next.astype(jnp.int32)
             + (~relay).astype(jnp.int32) + (holders - 1)
             + (r > 0).astype(jnp.int32) + (r < n_rows - 1).astype(jnp.int32))
    pl.semaphore_wait(barrier, known)

    def step(j):
        @pl.when(hi > 0)
        def _():
            z_copy(j).wait_recv()

        @pl.when(feeds_next)
        def _():
            z_copy(j).start()

        @pl.when(feeds_back)
        def _():
            z_back(j).start()

        for d in range(1, holders):
            x_copy(d, j).start()

        i = j - lag

        @pl.when((i >= 0) & (i < n_right))
        def _():
            @pl.when(r > 0)
            def _():
                r_copy(i).wait_recv()

            @pl.when(r < n_rows - 1)
            def _():
                r_copy(i).start()

        @pl.when(j + 1 < n_adj)
        def _():
            adj_copy(j + 1).wait()

        @pl.when((hi == 0) & (j + ahead < n_chunks))
        def _():
            convert_left(j + ahead)

        @pl.when((r == 0) & (j + 1 < n_right))
        def _():
            convert_right(j + 1)

    def compute(u):
        g = u // n_tiles
        t = lax.rem(u, n_tiles)

        @pl.when(t == 0)
        def _():
            for d in range(1, holders):
                @pl.loop(0, per_group)
                def _(k):
                    x_arrival(d, g * per_group + k).wait_recv()

        rows = pl.ds(pl.multiple_of(g * GROUP, GROUP), GROUP)
        cols = pl.ds(pl.multiple_of(t * TILE, TILE), TILE)
        counts = jnp.zeros((GROUP, TILE), jnp.float32)
        for h in range(holders):
            counts += jnp.dot(left[h, rows, :], right[h * block_cols:(h + 1) * block_cols, cols],
                              preferred_element_type=jnp.float32)
        out[rows, cols] = jnp.where(counts > 0.5, 1, adj[rows, cols]).astype(out.dtype)

    body_units = units - n_tiles
    ready = n_right - 1 + lag_of(n_rows - 1)
    first = min(n_chunks, max(ready, n_chunks - 2 - -(-body_units // PER_STEP)))
    done = min(body_units, PER_STEP * (n_chunks - first))
    done -= done % PER_STEP

    @pl.loop(0, first)
    def _(j):
        step(j)

    @pl.loop(first, n_chunks)
    def _(j):
        step(j)
        for p in range(PER_STEP):
            u = (j - first) * PER_STEP + p

            @pl.when(u < done)
            def _():
                compute(u)

    @pl.loop(n_chunks, max(n_chunks, ready + 1))
    def _(j):
        i = j - lag

        @pl.when((i >= 0) & (i < n_right))
        def _():
            @pl.when(r > 0)
            def _():
                r_copy(i).wait_recv()

            @pl.when(r < n_rows - 1)
            def _():
                r_copy(i).start()

    @pl.loop(done, body_units)
    def _(u):
        compute(u)

    def arrived(start):
        for d in range(1, holders):
            @pl.loop(start // CHUNK, (start + TAIL) // CHUNK)
            def _(k):
                x_arrival(d, k).wait_recv()

    def half(h, start, cols):
        rights = pl.ds(pl.multiple_of(h * block_cols, block_cols), block_cols)
        return jnp.dot(left[h, start:start + TAIL, :], right[rights, cols], preferred_element_type=jnp.float32)

    tiles = [slice(t * TILE, (t + 1) * TILE) for t in range(n_tiles)]
    for start in range(block_rows - GROUP, block_rows, TAIL):
        last = start + TAIL == block_rows
        if not last:
            arrived(start)
        for cols in tiles:
            partial[:, cols] = half(lo, start, cols)
        if last:
            arrived(start)
        for cols in tiles:
            counts = partial[:, cols]
            for d in range(1, holders):
                counts += half(lax.rem(lo + holders - d, holders), start, cols)
            out[start:start + TAIL, cols] = jnp.where(
                counts > 0.5, 1, adj[start:start + TAIL, cols]).astype(out.dtype)

    whole = left.at[lo]

    @pl.when(feeds_next)
    def _():
        pltpu.make_async_remote_copy(
            src_ref=whole, dst_ref=whole, send_sem=z_send, recv_sem=z_recv.at[0],
            device_id={"col": next_col}, device_id_type=MESH).wait_send()

    @pl.when(feeds_back)
    def _():
        pltpu.make_async_remote_copy(
            src_ref=whole, dst_ref=whole, send_sem=b_send, recv_sem=z_recv.at[0],
            device_id={"col": back_col}, device_id_type=MESH).wait_send()

    for d in range(1, holders):
        pltpu.make_async_remote_copy(
            src_ref=whole, dst_ref=whole, send_sem=x_send.at[d - 1], recv_sem=x_recv.at[d - 1, 0],
            device_id={"col": hi * holders + lax.rem(lo + d, holders)}, device_id_type=MESH).wait_send()

    @pl.when(r < n_rows - 1)
    def _():
        pltpu.make_async_remote_copy(
            src_ref=right, dst_ref=right, send_sem=r_send, recv_sem=r_recv.at[0],
            device_id={"row": r + 1}, device_id_type=MESH).wait_send()


def per_device(n_rows, n_cols, adjacency):
    block_rows, block_cols = adjacency.shape
    window = PANELS * PANEL
    holders = window // block_cols
    n_chunks = block_rows // CHUNK
    dma = pltpu.SemaphoreType.DMA
    closed = pl.pallas_call(
        functools.partial(kernel, n_rows, n_cols, window),
        out_shape=pltpu.VMEM((block_rows, block_cols), jnp.bfloat16),
        in_specs=[pl.BlockSpec(memory_space=pltpu.HBM)],
        out_specs=pl.BlockSpec(memory_space=pltpu.VMEM),
        scratch_shapes=[
            pltpu.VMEM((block_rows, block_cols), jnp.int32),
            pltpu.VMEM((holders, block_rows, block_cols), jnp.bfloat16),
            pltpu.VMEM((window, block_cols), jnp.bfloat16),
            pltpu.VMEM((TAIL, block_cols), jnp.float32),
            dma((block_rows // RIGHT,)),
            dma,
            dma,
            dma((n_chunks,)),
            dma((holders - 1,)),
            dma((holders - 1, n_chunks)),
            dma,
            dma((window // RIGHT,)),
        ],
        compiler_params=pltpu.CompilerParams(
            collective_id=0, has_side_effects=True, vmem_limit_bytes=40 * 1024 * 1024),
    )(pltpu.with_memory_space_constraint(adjacency, pltpu.HBM))
    return closed


def solution(mesh):
    spec = P("row", "col")
    return jax.shard_map(
        functools.partial(per_device, mesh.shape["row"], mesh.shape["col"]),
        mesh=mesh, in_specs=(spec,), out_specs=spec, check_vma=False)
```

profile of v0, /device:TPU:12, one launch (start us, length us, event | category | flops | bytes accessed | tf_op | source)
XLA Modules:
  0.0 105.5 jit_solution(15914776235213862271)
XLA Ops:
  0.0 103.5 %shard_map.17 = bf16[2048,1024]{1,0:T(8,128)(2,1)S(1)} custom-call(s32[2048,1024]{1,0:T(8,128)} %adj_hbm.1), custom_call_target="tpu_custom_call" | custom-call | tf_op jit(solution)/shard_map/pallas_call | solution.py:310
  103.5 2.0 %copy.3 = bf16[2048,1024]{1,0:T(8,128)(2,1)} copy(bf16[2048,1024]{1,0:T(8,128)(2,1)S(1)} %shard_map.17) | data formatting | bytes 8388608
where the time goes:
time: 106 us; the launch traced here: 105 us
  Pallas kernels  103 us (97%)
  local copies, waits for them, and re-layouts  2.02 us (2%)
    pallas_call x1, Pallas kernels, per_device(): pl.pallas_call(functools.partial(kernel, n_rows, n_cols, window), out_sha...  103 us

commit v1 on v0

--- a/solution.py
+++ b/solution.py
@@ -10,31 +10,33 @@
 PANEL = 512
 PANELS = 4
 
-CHUNK = 32
-RIGHT = 64
+CHUNK = 16
+RIGHT = 128
+LOAD = 256
+FIRST = 64
 GROUP = 256
 TAIL = 128
 TILE = 512
-PER_STEP = 1
+UNIT = 256
+RING = 32
+CREDIT = 16
+PACE = RIGHT // (2 * CHUNK)
 MESH = pl.DeviceIdType.MESH
 
 
 def lag_of(row):
-    return 1 + (5 * row) // 2
+    return PACE * (1 + row) + (3 * PACE // 2) * (row // 2)
 
 
 def kernel(n_rows, n_cols, window, adj_hbm, out, adj, left, right, partial,
-           adj_sem, z_send, b_send, z_recv, x_send, x_recv, r_send, r_recv):
+           adj_sem, z_send, b_send, z_recv, x_send, x_recv, r_send, r_recv, credit):
     block_rows, block_cols = adj.shape
     holders = left.shape[0]
     stages = n_cols // holders
     n_chunks = block_rows // CHUNK
-    n_adj = block_rows // RIGHT
     n_right = window // RIGHT
-    n_groups = block_rows // GROUP
-    n_tiles = block_cols // TILE
-    units = n_groups * n_tiles
-    per_group = GROUP // CHUNK
+    n_units = block_cols // UNIT
+    per_tail = TAIL // CHUNK
 
     r = lax.axis_index("row")
     c = lax.axis_index("col")
@@ -48,9 +50,18 @@
     next_col = c + holders * (1 + (hi + 2 < stages).astype(jnp.int32))
     back_col = c - holders
 
-    def adj_copy(i):
-        rows = pl.ds(pl.multiple_of(i * RIGHT, RIGHT), RIGHT)
-        return pltpu.make_async_copy(adj_hbm.at[rows], adj.at[rows], adj_sem.at[i])
+    source = jnp.where(relay, c - 2 * holders, jnp.where(hi == stages - 1, back_col, c + holders))
+    as_next = relay | (hi == stages - 1)
+
+    def adj_copy(start, size, sem):
+        rows = pl.ds(pl.multiple_of(start, CHUNK), size)
+        return pltpu.make_async_copy(adj_hbm.at[rows], adj.at[rows], adj_sem.at[sem])
+
+    def adj_load(i):
+        return adj_copy(i * LOAD, LOAD, i + 1)
+
+    head = adj_copy(0, FIRST, 0)
+    neck = adj_copy(FIRST, LOAD - FIRST, 1)
 
     def chunk(j):
         return pl.ds(pl.multiple_of(j * CHUNK, CHUNK), CHUNK)
@@ -58,27 +69,27 @@
     def z_copy(j):
         part = left.at[lo, chunk(j)]
         return pltpu.make_async_remote_copy(
-            src_ref=part, dst_ref=part, send_sem=z_send, recv_sem=z_recv.at[j],
+            src_ref=part, dst_ref=part, send_sem=z_send, recv_sem=z_recv.at[lax.rem(j, RING)],
             device_id={"col": next_col}, device_id_type=MESH)
 
     def z_back(j):
         part = left.at[lo, chunk(j)]
         return pltpu.make_async_remote_copy(
-            src_ref=part, dst_ref=part, send_sem=b_send, recv_sem=z_recv.at[j],
+            src_ref=part, dst_ref=part, send_sem=b_send, recv_sem=z_recv.at[lax.rem(j, RING)],
             device_id={"col": back_col}, device_id_type=MESH)
 
     def x_copy(d, j):
         part = left.at[lo, chunk(j)]
         peer = hi * holders + lax.rem(lo + d, holders)
         return pltpu.make_async_remote_copy(
-            src_ref=part, dst_ref=part, send_sem=x_send.at[d - 1], recv_sem=x_recv.at[d - 1, j],
+            src_ref=part, dst_ref=part, send_sem=x_send.at[d - 1], recv_sem=x_recv.at[d - 1, j // per_tail],
             device_id={"col": peer}, device_id_type=MESH)
 
-    def x_arrival(d, j):
-        part = left.at[lax.rem(lo + holders - d, holders), chunk(j)]
+    def x_arrival(d, i):
+        part = left.at[lax.rem(lo + holders - d, holders), pl.ds(pl.multiple_of(i * TAIL, TAIL), TAIL)]
         peer = hi * holders + lax.rem(lo + holders - d, holders)
         return pltpu.make_async_remote_copy(
-            src_ref=part, dst_ref=part, send_sem=x_send.at[d - 1], recv_sem=x_recv.at[d - 1, j],
+            src_ref=part, dst_ref=part, send_sem=x_send.at[d - 1], recv_sem=x_recv.at[d - 1, i],
             device_id={"col": peer}, device_id_type=MESH)
 
     def r_rows(i):
@@ -90,7 +101,7 @@
             src_ref=part, dst_ref=part, send_sem=r_send, recv_sem=r_recv.at[i],
             device_id={"row": r + 1}, device_id_type=MESH)
 
-    adj_copy(0).start()
+    head.start()
 
     barrier = pltpu.get_barrier_semaphore()
 
@@ -131,91 +142,113 @@
     def convert_right(i):
         right[r_rows(i), :] = adj[r_rows(i), :].astype(jnp.bfloat16)
 
-    ahead = RIGHT // CHUNK
-    adj_copy(0).wait()
-
-    @pl.loop(1, n_adj)
+    ahead = FIRST // CHUNK
+    neck.start()
+
+    @pl.loop(1, block_rows // LOAD)
     def _(i):
-        adj_copy(i).start()
+        adj_load(i).start()
+
+    head.wait()
 
     @pl.when(hi == 0)
     def _():
         for k in range(ahead):
             convert_left(k)
-
-    @pl.when(r == 0)
-    def _():
-        convert_right(0)
 
     known = (2 * feeds_back.astype(jnp.int32) + feeds_next.astype(jnp.int32)
              + (~relay).astype(jnp.int32) + (holders - 1)
              + (r > 0).astype(jnp.int32) + (r < n_rows - 1).astype(jnp.int32))
     pl.semaphore_wait(barrier, known)
 
+    def paid(j):
+        return (lax.rem(j, CREDIT) == 0) & (j >= RING)
+
+    def pass_right(j):
+        late = j - lag
+        i = late // PACE
+
+        @pl.when((late >= 0) & (lax.rem(late, PACE) == 0) & (i < n_right))
+        def _():
+            @pl.when(r > 0)
+            def _():
+                r_copy(i).wait_recv()
+
+            @pl.when(r < n_rows - 1)
+            def _():
+                r_copy(i).start()
+
     def step(j):
         @pl.when(hi > 0)
         def _():
             z_copy(j).wait_recv()
 
+            @pl.when((lax.rem(j + 1, CREDIT) == 0) & (j + 1 <= n_chunks - RING))
+            def _():
+                pl.semaphore_signal(credit.at[jnp.where(as_next, 0, 1)], inc=1,
+                                    device_id={"col": source}, device_id_type=MESH)
+
         @pl.when(feeds_next)
         def _():
+            @pl.when(paid(j))
+            def _():
+                pl.semaphore_wait(credit.at[0], 1)
+
             z_copy(j).start()
 
         @pl.when(feeds_back)
         def _():
+            @pl.when(paid(j))
+            def _():
+                pl.semaphore_wait(credit.at[1], 1)
+
             z_back(j).start()
 
         for d in range(1, holders):
             x_copy(d, j).start()
 
-        i = j - lag
-
-        @pl.when((i >= 0) & (i < n_right))
-        def _():
-            @pl.when(r > 0)
-            def _():
-                r_copy(i).wait_recv()
-
-            @pl.when(r < n_rows - 1)
-            def _():
-                r_copy(i).start()
-
-        @pl.when(j + 1 < n_adj)
-        def _():
-            adj_copy(j + 1).wait()
+        pass_right(j)
+
+        @pl.when(j == 0)
+        def _():
+            neck.wait()
+
+        per_load = 2 * PACE * LOAD // (2 * RIGHT)
+
+        @pl.when((j > 0) & (lax.rem(j, per_load) == 0) & (j < per_load * (block_rows // LOAD)))
+        def _():
+            adj_load(j // per_load).wait()
 
         @pl.when((hi == 0) & (j + ahead < n_chunks))
         def _():
             convert_left(j + ahead)
 
-        @pl.when((r == 0) & (j + 1 < n_right))
-        def _():
-            convert_right(j + 1)
+        @pl.when((r == 0) & (lax.rem(j, PACE) == 0) & (j < PACE * n_right))
+        def _():
+            convert_right(j // PACE)
 
     def compute(u):
-        g = u // n_tiles
-        t = lax.rem(u, n_tiles)
+        g = u // n_units
+        t = lax.rem(u, n_units)
 
         @pl.when(t == 0)
         def _():
             for d in range(1, holders):
-                @pl.loop(0, per_group)
-                def _(k):
-                    x_arrival(d, g * per_group + k).wait_recv()
+                for k in range(GROUP // TAIL):
+                    x_arrival(d, g * (GROUP // TAIL) + k).wait_recv()
 
         rows = pl.ds(pl.multiple_of(g * GROUP, GROUP), GROUP)
-        cols = pl.ds(pl.multiple_of(t * TILE, TILE), TILE)
-        counts = jnp.zeros((GROUP, TILE), jnp.float32)
+        cols = pl.ds(pl.multiple_of(t * UNIT, UNIT), UNIT)
+        counts = jnp.zeros((GROUP, UNIT), jnp.float32)
         for h in range(holders):
             counts += jnp.dot(left[h, rows, :], right[h * block_cols:(h + 1) * block_cols, cols],
                               preferred_element_type=jnp.float32)
         out[rows, cols] = jnp.where(counts > 0.5, 1, adj[rows, cols]).astype(out.dtype)
 
-    body_units = units - n_tiles
-    ready = n_right - 1 + lag_of(n_rows - 1)
-    first = min(n_chunks, max(ready, n_chunks - 2 - -(-body_units // PER_STEP)))
-    done = min(body_units, PER_STEP * (n_chunks - first))
-    done -= done % PER_STEP
+    body_units = (block_rows // GROUP - 1) * n_units
+    ready = PACE * (n_right - 1) + lag_of(n_rows - 1)
+    first = min(n_chunks, max(ready, n_chunks - 4 - body_units))
+    done = min(body_units, n_chunks - first)
 
     @pl.loop(0, first)
     def _(j):
@@ -224,26 +257,14 @@
     @pl.loop(first, n_chunks)
     def _(j):
         step(j)
-        for p in range(PER_STEP):
-            u = (j - first) * PER_STEP + p
-
-            @pl.when(u < done)
-            def _():
-                compute(u)
+
+        @pl.when(j - first < done)
+        def _():
+            compute(j - first)
 
     @pl.loop(n_chunks, max(n_chunks, ready + 1))
     def _(j):
-        i = j - lag
-
-        @pl.when((i >= 0) & (i < n_right))
-        def _():
-            @pl.when(r > 0)
-            def _():
-                r_copy(i).wait_recv()
-
-            @pl.when(r < n_rows - 1)
-            def _():
-                r_copy(i).start()
+        pass_right(j)
 
     @pl.loop(done, body_units)
     def _(u):
@@ -251,15 +272,13 @@
 
     def arrived(start):
         for d in range(1, holders):
-            @pl.loop(start // CHUNK, (start + TAIL) // CHUNK)
-            def _(k):
-                x_arrival(d, k).wait_recv()
+            x_arrival(d, start // TAIL).wait_recv()
 
     def half(h, start, cols):
         rights = pl.ds(pl.multiple_of(h * block_cols, block_cols), block_cols)
         return jnp.dot(left[h, start:start + TAIL, :], right[rights, cols], preferred_element_type=jnp.float32)
 
-    tiles = [slice(t * TILE, (t + 1) * TILE) for t in range(n_tiles)]
+    tiles = [slice(t, t + TILE) for t in range(0, block_cols, TILE)]
     for start in range(block_rows - GROUP, block_rows, TAIL):
         last = start + TAIL == block_rows
         if not last:
@@ -305,7 +324,6 @@
     block_rows, block_cols = adjacency.shape
     window = PANELS * PANEL
     holders = window // block_cols
-    n_chunks = block_rows // CHUNK
     dma = pltpu.SemaphoreType.DMA
     closed = pl.pallas_call(
         functools.partial(kernel, n_rows, n_cols, window),
@@ -317,14 +335,15 @@
             pltpu.VMEM((holders, block_rows, block_cols), jnp.bfloat16),
             pltpu.VMEM((window, block_cols), jnp.bfloat16),
             pltpu.VMEM((TAIL, block_cols), jnp.float32),
-            dma((block_rows // RIGHT,)),
+            dma((block_rows // LOAD + 1,)),
             dma,
             dma,
-            dma((n_chunks,)),
+            dma((RING,)),
             dma((holders - 1,)),
-            dma((holders - 1, n_chunks)),
+            dma((holders - 1, block_rows // TAIL)),
             dma,
             dma((window // RIGHT,)),
+            pltpu.SemaphoreType.REGULAR((2,)),
         ],
         compiler_params=pltpu.CompilerParams(
             collective_id=0, has_side_effects=True, vmem_limit_bytes=40 * 1024 * 1024),

time: 106 us -> 104 us (0.981)
    pallas_call x1, Pallas kernels: 103 us -> 102 us  [per_device(): pl.pallas_call(functools.partial(kernel, n_rows, n_cols, window), out_sha...]
where the time goes in v1:
time: 104 us
  Pallas kernels  102 us (98%)
  local copies, waits for them, and re-layouts  2.02 us (2%)
    pallas_call x1, Pallas kernels, per_device(): pl.pallas_call(functools.partial(kernel, n_rows, n_cols, window), out_sha...  102 us

profile of v1, /device:TPU:12, one launch (start us, length us, event | category | flops | bytes accessed | tf_op | source)
XLA Modules:
  0.0 103.5 jit_solution(12937236315690450762)
XLA Ops:
  0.0 101.5 %shard_map.17 = bf16[2048,1024]{1,0:T(8,128)(2,1)S(1)} custom-call(s32[2048,1024]{1,0:T(8,128)} %adj_hbm.1), custom_call_target="tpu_custom_call" | custom-call | tf_op jit(solution)/shard_map/pallas_call | solution.py:328
  101.5 2.0 %copy.3 = bf16[2048,1024]{1,0:T(8,128)(2,1)} copy(bf16[2048,1024]{1,0:T(8,128)(2,1)S(1)} %shard_map.17) | data formatting | bytes 8388608
